TPU v7x, 32 devices: a whole 2x2x4 slice. The times are simulated.
32 devices in a mesh: gx: 4 (over y, core), gy: 8 (over z, x).
Axes of the slice: x: 2, y: 2, z: 4, core: 2. Of those that a mesh axis runs over, the one named last changes fastest.
Arguments:
- old_master: float32 [32, 128, 1536], P('gx', 'gy'), may hold values from -3 to 3
- old_first: float32 [32, 128, 1536], P('gx', 'gy'), may hold values from -3 to 3
- old_second: float32 [32, 128, 1536], P('gx', 'gy'), may hold values from 0.01 to 1
- new_grad: bfloat16 [32, 128, 1536], P(('gx', 'gy')), may hold values from -3072 to 3072
- counts: int32 [32, 32], P(None, ('gx', 'gy')), may hold values from 1 to 72, as said below
- old_owner: int32 [32], replicated, may hold values from 0 to 31, each once
- new_owner: int32 [32], replicated, may hold values from 0 to 31, each once
Outputs:
- new_master: float32 [32, 128, 1536], P(('gx', 'gy'))
- new_first: float32 [32, 128, 1536], P(('gx', 'gy'))
- new_second: float32 [32, 128, 1536], P(('gx', 'gy'))
Inputs may be any that keep to these rules, and one draw needn't show every extreme that they name: `old_owner`: every number of 0 to 31 appears once. `new_owner`: every number of 0 to 31 appears once. `counts`: every device routed at least one token to every expert.
All inputs are finite; a program needn't handle non-finite values.
Results may differ from a plain program's by a relative error of at most 0.0003.
Values sent between devices are 32-bit elements; how exact they have to be, the bound alone decides.
A program may use at most 64 MiB of HBM per device.

v0:
```python
import jax
import jax.numpy as jnp
from jax import lax
from jax.sharding import PartitionSpec as P

first_correction = 1.0 - 0.9**10
second_correction = 1.0 - 0.999**10


def adam_step(master, first, second, grad, slot_count):
    scaled = grad.astype(jnp.float32) / slot_count
    new_first = 0.9 * first + 0.1 * scaled
    new_second = 0.999 * second + 0.001 * scaled * scaled
    step_dir = new_first / first_correction / (jnp.sqrt(new_second / second_correction) + 1e-08)
    new_master = master - 0.01 * (step_dir + 0.1 * master)
    return (new_master, new_first, new_second)


def reorder(block, groups_x, groups_y):
    total_rows = block.shape[1]
    piece = total_rows // (groups_x * groups_y)
    shaped = block.reshape(1, groups_x, groups_y, piece, block.shape[2])
    return shaped.transpose(0, 2, 1, 3, 4).reshape(1, total_rows, block.shape[2])


def body(old_master, old_first, old_second, new_grad, counts, old_owner, new_owner):
    experts = old_owner.shape[0]
    groups_x = lax.axis_size("gx")
    groups_y = lax.axis_size("gy")
    my_slot = lax.axis_index("gx") * groups_y + lax.axis_index("gy")
    slots = jnp.arange(experts, dtype=jnp.int32)
    onehot = new_owner[:, None] == slots[None, :]
    source = jnp.sum(jnp.where(onehot, old_owner[:, None], 0), axis=0)
    local_counts = counts[:, 0].astype(jnp.float32)
    by_rows = (
        lax.all_to_all(old_master, "gx", split_axis=1, concat_axis=0, tiled=True),
        lax.all_to_all(old_first, "gx", split_axis=1, concat_axis=0, tiled=True),
        lax.all_to_all(old_second, "gx", split_axis=1, concat_axis=0, tiled=True),
    )
    permuted = tuple((jnp.take(state, source, axis=0) for state in by_rows))
    landed = lax.all_to_all(permuted, ("gx", "gy"), split_axis=0, concat_axis=1, tiled=True)
    arrived = tuple((reorder(state, groups_x, groups_y) for state in landed))
    totals = lax.psum(local_counts, ("gx", "gy"))
    slot_count = jnp.sum(jnp.where(new_owner == my_slot, totals, jnp.float32(0.0)))
    return adam_step(arrived[0], arrived[1], arrived[2], new_grad, slot_count)


def solution(mesh):
    placed = (
        P("gx", "gy", None),
        P("gx", "gy", None),
        P("gx", "gy", None),
        P(("gx", "gy"), None, None),
        P(None, ("gx", "gy")),
        P(),
        P(),
    )
    return jax.shard_map(
        body,
        mesh=mesh,
        in_specs=placed,
        out_specs=(
            P(("gx", "gy"), None, None),
            P(("gx", "gy"), None, None),
            P(("gx", "gy"), None, None),
        ),
        check_vma=False,
    )
```

profile of v0, /device:TPU:0, one launch (start us, length us, event | category | flops | bytes accessed | tf_op | source)
XLA Modules:
  0.0 156.1 jit_solution(17211418162359433335)
XLA Ops:
  0.6 2.5 %copy.67 = f32[8,16,1536]{2,0,1:T(8,128)} copy(f32[8,16,1536]{2,1,0:T(8,128)} %param.9) | data formatting | bytes 1572864 | tf_op args[0]
  3.1 4.4 %all-to-all-start = ((f32[8,16,1536]{2,0,1:T(8,128)}), f32[8,16,1536]{2,0,1:T(8,128)S(1)}, u32[]{:S(2)}, u32[]{:S(2)}) async-start(f32[8,16,1536]{2,0,1:T(8,128)} %copy.67), calls=%async_computation | async-start | bytes 1572864 | tf_op jit(solution)/shard_map/all_to_all | solution.py:36
  7.5 1.3 copy.72
  8.8 10.3 %all-to-all-done = f32[8,16,1536]{2,0,1:T(8,128)S(1)} async-done(((f32[8,16,1536]{2,0,1:T(8,128)}), f32[8,16,1536]{2,0,1:T(8,128)S(1)}, u32[]{:S(2)}, u32[]{:S(2)}) %all-to-all-start) | async-done | bytes 786464 | tf_op jit(solution)/shard_map/all_to_all | solution.py:36
  19.1 3.5 %all-to-all-start.2 = ((f32[8,16,1536]{2,0,1:T(8,128)}), f32[8,16,1536]{2,0,1:T(8,128)S(1)}, u32[]{:S(2)}, u32[]{:S(2)}) async-start(f32[8,16,1536]{2,0,1:T(8,128)} %copy.72), calls=%async_computation.2 | async-start | bytes 1572864 | tf_op jit(solution)/shard_map/all_to_all | solution.py:37
  22.6 1.3 copy.78
  24.0 10.2 %all-to-all-done.2 = f32[8,16,1536]{2,0,1:T(8,128)S(1)} async-done(((f32[8,16,1536]{2,0,1:T(8,128)}), f32[8,16,1536]{2,0,1:T(8,128)S(1)}, u32[]{:S(2)}, u32[]{:S(2)}) %all-to-all-start.2) | async-done | bytes 786464 | tf_op jit(solution)/shard_map/all_to_all | solution.py:37
  34.2 3.5 %all-to-all-start.4 = ((f32[8,16,1536]{2,0,1:T(8,128)}), f32[8,16,1536]{2,0,1:T(8,128)S(1)}, u32[]{:S(2)}, u32[]{:S(2)}) async-start(f32[8,16,1536]{2,0,1:T(8,128)} %copy.78), calls=%async_computation.4 | async-start | bytes 1572864 | tf_op jit(solution)/shard_map/all_to_all | solution.py:38
  37.7 0.1 select_reduce_fusion
  37.9 0.1 copy.104
  37.9 0.5 copy.69
  38.4 0.1 copy.102
  38.5 1.4 copy.74
  39.9 1.0 gather_fusion
  40.9 2.2 %gather_fusion.1 = f32[32,4,1536]{2,1,0:T(4,128)S(1)} fusion(f32[32,4,1536]{2,1,0:T(4,128)} %copy.74, s32[1024]{0:T(1024)S(1)} %pad_clamp_fusion), kind=kCustom, calls=%fused_computation.1.clone | custom fusion | bytes 1572992 | tf_op jit(solution)/shard_map/jit(_take)/gather | solution.py:40
  43.1 6.2 %all-to-all-done.4 = f32[8,16,1536]{2,0,1:T(8,128)S(1)} async-done(((f32[8,16,1536]{2,0,1:T(8,128)}), f32[8,16,1536]{2,0,1:T(8,128)S(1)}, u32[]{:S(2)}, u32[]{:S(2)}) %all-to-all-start.4) | async-done | bytes 786464 | tf_op jit(solution)/shard_map/all_to_all | solution.py:38
  49.4 0.5 copy.80
  49.9 1.0 gather_fusion.2
  50.9 1.5 broadcast_select_fusion
  52.4 27.2 %all_to_all.81 = f32[32,4,1536]{2,1,0:T(4,128)S(1)} all-to-all(f32[32,4,1536]{2,1,0:T(4,128)S(1)} %get-tuple-element.13), channel_id=1, replica_groups=mesh['gx'=4,'gy'=8] {'gx','gy'}, dimensions={0} | all-to-all | bytes 1572864 | tf_op jit(solution)/shard_map/all_to_all | solution.py:41
  79.6 24.0 %all_to_all.82 = f32[32,4,1536]{2,1,0:T(4,128)S(1)} all-to-all(f32[32,4,1536]{2,1,0:T(4,128)S(1)} %get-tuple-element.14), channel_id=1, replica_groups=mesh['gx'=4,'gy'=8] {'gx','gy'}, dimensions={0} | all-to-all | bytes 1572864 | tf_op jit(solution)/shard_map/all_to_all | solution.py:41
  103.6 2.8 %all-to-all-start.1 = ((f32[32,4,1536]{2,1,0:T(4,128)}), f32[32,4,1536]{2,1,0:T(4,128)S(1)}, u32[]{:S(2)}, u32[]{:S(2)}) async-start(f32[32,4,1536]{2,1,0:T(4,128)} %get-tuple-element.15), calls=%async_computation.1 | async-start | bytes 1572864 | tf_op jit(solution)/shard_map/all_to_all | solution.py:41
  106.4 43.1 %psum.7 = f32[32]{0:T(128)S(1)} all-reduce(f32[32]{0:T(128)S(1)} %convert_bitcast_fusion), channel_id=1, replica_groups=mesh['gx'=4,'gy'=8] {'gx','gy'}, use_global_device_ids=true, to_apply=%region_1.3 | all-reduce | flops 32 | bytes 256 | tf_op jit(solution)/shard_map/psum | solution.py:43
  149.5 0.7 fusion.3
  150.2 0.3 fusion.1
  150.5 0.8 copy.82
  151.3 0.3 fusion.2
  151.6 0.8 copy.76
  152.4 0.3 copy.103
  152.7 0.8 copy.71
  153.5 0.2 copy-done.2
  153.7 2.5 %multiply_subtract_fusion = (f32[1,128,1536]{2,1,0:T(8,128)}, f32[1,128,1536]{2,1,0:T(8,128)}, f32[1,128,1536]{2,1,0:T(8,128)}) fusion(f32[1,128,1536]{2,0,1:T(1,128)S(1)} %bitcast.45, f32[]{:T(128)} %fusion.3, bf16[1,128,1536]{2,1,0:T(8,128)(2,1)S(1)} %copy-done.2, f32[1,128,1536]{2,0,1:T(1,128)S(1)} %bitcast.44, f32[1,128,1536]{2,0,1:T(1,128)S(1)} %bitcast.43), kind=kLoop, calls=%fused_computation.14 | loop fusion | flops 2949120 | bytes 5111812 | tf_op jit(solution)/shard_map/sub | solution.py:15
  (17 shorter events, 0.1 us)
Async XLA Ops:
  3.1 4.4 %copy-start = (f32[8,16,1536]{2,1,0:T(8,128)S(1)}, f32[8,16,1536]{2,1,0:T(8,128)}, u32[]{:S(2)}) copy-start(f32[8,16,1536]{2,1,0:T(8,128)} %param.10) | copy-start | bytes 2359300
  3.1 16.0 %all-to-all-start = ((f32[8,16,1536]{2,0,1:T(8,128)}), f32[8,16,1536]{2,0,1:T(8,128)S(1)}, u32[]{:S(2)}, u32[]{:S(2)}) async-start(f32[8,16,1536]{2,0,1:T(8,128)} %copy.67), calls=%async_computation | async-start | bytes 1572864 | tf_op jit(solution)/shard_map/all_to_all | solution.py:36
  8.8 13.8 %copy-start.1 = (f32[8,16,1536]{2,1,0:T(8,128)S(1)}, f32[8,16,1536]{2,1,0:T(8,128)}, u32[]{:S(2)}) copy-start(f32[8,16,1536]{2,1,0:T(8,128)} %param.11) | copy-start | bytes 2359300
  19.1 15.1 %all-to-all-start.2 = ((f32[8,16,1536]{2,0,1:T(8,128)}), f32[8,16,1536]{2,0,1:T(8,128)S(1)}, u32[]{:S(2)}, u32[]{:S(2)}) async-start(f32[8,16,1536]{2,0,1:T(8,128)} %copy.72), calls=%async_computation.2 | async-start | bytes 1572864 | tf_op jit(solution)/shard_map/all_to_all | solution.py:37
  24.0 13.7 %copy-start.3 = (s32[32]{0:T(128)S(1)}, s32[32]{0:T(128)}, u32[]{:S(2)}) copy-start(s32[32]{0:T(128)} %param.15) | copy-start | bytes 388
  24.0 13.8 %copy-start.4 = (s32[32]{0:T(128)S(1)}, s32[32]{0:T(128)}, u32[]{:S(2)}) copy-start(s32[32]{0:T(128)} %param.14) | copy-start | bytes 388
  34.2 15.1 %all-to-all-start.4 = ((f32[8,16,1536]{2,0,1:T(8,128)}), f32[8,16,1536]{2,0,1:T(8,128)S(1)}, u32[]{:S(2)}, u32[]{:S(2)}) async-start(f32[8,16,1536]{2,0,1:T(8,128)} %copy.78), calls=%async_computation.4 | async-start | bytes 1572864 | tf_op jit(solution)/shard_map/all_to_all | solution.py:38
  103.6 2.8 %copy-start.5 = (s32[32,1]{0,1:T(1,128)S(1)}, s32[32,1]{0,1:T(1,128)}, u32[]{:S(2)}) copy-start(s32[32,1]{0,1:T(1,128)} %param.13) | copy-start | bytes 388
  103.6 48.8 %all-to-all-start.1 = ((f32[32,4,1536]{2,1,0:T(4,128)}), f32[32,4,1536]{2,1,0:T(4,128)S(1)}, u32[]{:S(2)}, u32[]{:S(2)}) async-start(f32[32,4,1536]{2,1,0:T(4,128)} %get-tuple-element.15), calls=%async_computation.1 | async-start | bytes 1572864 | tf_op jit(solution)/shard_map/all_to_all | solution.py:41
  152.7 1.0 copy-start.2
where the time goes:
time: 157 us; the launch traced here: 156 us
  blocking collectives  94.3 us (60%)
  waiting for transfers between devices  26.7 us (17%)
  local copies, waits for them, and re-layouts  14.8 us (9%)
  starting transfers between devices  14.1 us (9%)
  other arithmetic  5.31 us (3%)
    all_to_all x2, blocking collectives, body(): lax.all_to_all(permuted, ('gx', 'gy'), split_axis=0, concat_axis=1, tiled...  51.2 us
    psum x1, blocking collectives, body(): totals = lax.psum(local_counts, ('gx', 'gy'))  43.1 us
    all_to_all x1, waiting for transfers between devices, body(): lax.all_to_all(old_master, 'gx', split_axis=1, concat_axis=0, tiled=True)  10.3 us
    all_to_all x1, waiting for transfers between devices, body(): lax.all_to_all(old_first, 'gx', split_axis=1, concat_axis=0, tiled=True)  10.2 us
    all_to_all x1, waiting for transfers between devices, body(): lax.all_to_all(old_second, 'gx', split_axis=1, concat_axis=0, tiled=True)  6.23 us
    unnamed x15, local copies, waits for them, and re-layouts  5.34 us
    all_to_all x1, starting transfers between devices, body(): lax.all_to_all(old_master, 'gx', split_axis=1, concat_axis=0, tiled=True)  4.4 us
    gather x3, local copies, waits for them, and re-layouts, body(): permuted = tuple((jnp.take(state, source, axis=0) for state in by_rows))  4.19 us
  transfers between devices with their start and end apart: 4, of which 3 were waited for; matrix products, arithmetic and copies ran while one was open for 7% of the time, Pallas kernels for 0%

commit v1 on v0

--- a/solution.py
+++ b/solution.py
@@ -1,10 +1,18 @@
+import functools
+
 import jax
 import jax.numpy as jnp
 from jax import lax
+from jax.experimental import pallas as pl
+from jax.experimental.pallas import tpu as pltpu
 from jax.sharding import PartitionSpec as P
 
 first_correction = 1.0 - 0.9**10
 second_correction = 1.0 - 0.999**10
+MESH = pl.DeviceIdType.MESH
+LANES = 128
+SUBLANES = 8
+SUBCHUNKS = 2
 
 
 def adam_step(master, first, second, grad, slot_count):
@@ -23,7 +31,7 @@
     return shaped.transpose(0, 2, 1, 3, 4).reshape(1, total_rows, block.shape[2])
 
 
-def body(old_master, old_first, old_second, new_grad, counts, old_owner, new_owner):
+def plain_body(old_master, old_first, old_second, new_grad, counts, old_owner, new_owner):
     experts = old_owner.shape[0]
     groups_x = lax.axis_size("gx")
     groups_y = lax.axis_size("gy")
@@ -32,10 +40,9 @@
     onehot = new_owner[:, None] == slots[None, :]
     source = jnp.sum(jnp.where(onehot, old_owner[:, None], 0), axis=0)
     local_counts = counts[:, 0].astype(jnp.float32)
-    by_rows = (
-        lax.all_to_all(old_master, "gx", split_axis=1, concat_axis=0, tiled=True),
-        lax.all_to_all(old_first, "gx", split_axis=1, concat_axis=0, tiled=True),
-        lax.all_to_all(old_second, "gx", split_axis=1, concat_axis=0, tiled=True),
+    by_rows = tuple(
+        lax.all_to_all(state, "gx", split_axis=1, concat_axis=0, tiled=True)
+        for state in (old_master, old_first, old_second)
     )
     permuted = tuple((jnp.take(state, source, axis=0) for state in by_rows))
     landed = lax.all_to_all(permuted, ("gx", "gy"), split_axis=0, concat_axis=1, tiled=True)
@@ -43,6 +50,192 @@
     totals = lax.psum(local_counts, ("gx", "gy"))
     slot_count = jnp.sum(jnp.where(new_owner == my_slot, totals, jnp.float32(0.0)))
     return adam_step(arrived[0], arrived[1], arrived[2], new_grad, slot_count)
+
+
+def rehome_kernel(dims, old_owner, new_owner, owner_row, count_row, old_m, old_f, old_s, *rest):
+    groups_x, groups_y, experts, held, rows, tiles, width, chunks = dims
+    outs, count_out = rest[:3], rest[3]
+    by_rows = rest[4 : 4 + chunks]
+    staged = rest[4 + chunks : 4 + 2 * chunks]
+    (source, all_counts, local_sem, send1, recv1, send2, recv2, send_c, recv_c) = rest[4 + 2 * chunks :]
+    olds = (old_m, old_f, old_s)
+    devices = groups_x * groups_y
+    per_state = chunks // 3
+    splits = groups_x // tiles
+    span = per_state * width
+    gx = lax.axis_index("gx")
+    gy = lax.axis_index("gy")
+    me = gx * groups_y + gy
+
+    def peer(i):
+        at = i // groups_x
+        sign = 1 - 2 * (at % 2)
+        off = groups_y // 2 + sign * ((at + 1) // 2)
+        px = (gx + i % groups_x) % groups_x
+        py = (gy + off) % groups_y
+        return px, py
+
+    def for_peers(fn):
+        def step(i, carry):
+            fn(*peer(i))
+            return carry
+
+        lax.fori_loop(0, devices - groups_x, step, 0)
+        lax.fori_loop(devices - groups_x + 1, devices, step, 0)
+
+    barrier = pltpu.get_barrier_semaphore()
+    for_peers(lambda px, py: pl.semaphore_signal(barrier, inc=1, device_id=(px, py), device_id_type=MESH))
+    pl.semaphore_wait(barrier, devices - 1)
+
+    def old_piece(chunk, part):
+        state, sub = chunk // per_state, chunk % per_state
+        row = pl.multiple_of((part // splits) * SUBLANES, SUBLANES)
+        col = pl.multiple_of((part % splits) * span + sub * width, LANES)
+        return olds[state].at[:, pl.ds(row, SUBLANES), pl.ds(col, width)]
+
+    def own_rows(chunk):
+        return by_rows[chunk].at[pl.ds(gx * held, held)]
+
+    def first_copy(chunk, off):
+        part = (gx + off) % groups_x
+        return pltpu.make_async_remote_copy(
+            src_ref=old_piece(chunk, part),
+            dst_ref=own_rows(chunk),
+            send_sem=send1.at[chunk, off],
+            recv_sem=recv1.at[chunk, off],
+            device_id=(part, gy),
+            device_id_type=MESH,
+        )
+
+    def local_copy(chunk):
+        return pltpu.make_async_copy(old_piece(chunk, gx), own_rows(chunk), local_sem.at[chunk])
+
+    order = [sub + state * per_state for sub in range(per_state) for state in range(3)]
+    for chunk in order:
+        for off in range(1, groups_x):
+            first_copy(chunk, off).start()
+        local_copy(chunk).start()
+
+    def count_copy(px, py):
+        return pltpu.make_async_remote_copy(
+            src_ref=count_row,
+            dst_ref=all_counts.at[me],
+            send_sem=send_c,
+            recv_sem=recv_c,
+            device_id=(px, py),
+            device_id_type=MESH,
+        )
+
+    for_peers(lambda px, py: count_copy(px, py).start())
+    all_counts[me] = count_row[...]
+
+    def find(slot, carry):
+        total = jnp.int32(0)
+        for e in range(experts):
+            total = total + jnp.where(new_owner[e] == slot, old_owner[e], 0)
+        source[slot] = total
+        return carry
+
+    lax.fori_loop(0, experts, find, 0)
+
+    def place(chunk):
+        state, sub = chunk // per_state, chunk % per_state
+        row = pl.multiple_of(gy * rows + (gx // splits) * SUBLANES, SUBLANES)
+        col = pl.multiple_of((gx % splits) * span + sub * width, LANES)
+        return state, row, col
+
+    for chunk in order:
+        local_copy(chunk).wait()
+        for off in range(1, groups_x):
+            first_copy(chunk, off).wait_recv()
+
+        def stage(slot, carry):
+            staged[chunk][slot] = by_rows[chunk][source[slot]]
+            return carry
+
+        lax.fori_loop(0, experts, stage, 0, unroll=4)
+        state, row, col = place(chunk)
+
+        def send(px, py):
+            pltpu.make_async_remote_copy(
+                src_ref=staged[chunk].at[px * groups_y + py],
+                dst_ref=outs[state].at[0, pl.ds(row, SUBLANES), pl.ds(col, width)],
+                send_sem=send2.at[chunk],
+                recv_sem=recv2.at[chunk],
+                device_id=(px, py),
+                device_id_type=MESH,
+            ).start()
+
+        for_peers(send)
+        outs[state][0, pl.ds(row, SUBLANES), pl.ds(col, width)] = by_rows[chunk][source[me]]
+
+    others = all_counts.at[pl.ds(0, devices - 1)]
+    pltpu.make_async_copy(others, others, recv_c).wait()
+    totals = jnp.sum(all_counts[...], axis=0)
+    count = jnp.sum(jnp.where(owner_row[...] == me, totals, 0.0), axis=1, keepdims=True)
+    count_out[...] = jnp.broadcast_to(count, count_out.shape)
+
+    for chunk in order:
+        for off in range(1, groups_x):
+            first_copy(chunk, off).wait_send()
+    pltpu.make_async_copy(others, others, send_c).wait()
+    for chunk in order:
+        sent = staged[chunk].at[pl.ds(0, devices - 1)]
+        pltpu.make_async_copy(sent, sent, send2.at[chunk]).wait()
+        pltpu.make_async_copy(sent, sent, recv2.at[chunk]).wait()
+
+
+def tiled_plan(groups_x, groups_y, shape, experts):
+    held, rows, cols = shape
+    if rows % SUBLANES or experts != groups_x * groups_y:
+        return None
+    tiles = rows // SUBLANES
+    if groups_x % tiles:
+        return None
+    span = cols // (groups_x // tiles)
+    if span % (LANES * SUBCHUNKS) or cols % span:
+        return None
+    return (groups_x, groups_y, experts, held, rows, tiles, span // SUBCHUNKS, 3 * SUBCHUNKS)
+
+
+def kernel_body(dims, old_master, old_first, old_second, new_grad, counts, old_owner, new_owner):
+    groups_x, groups_y, experts, held, rows, tiles, width, chunks = dims
+    devices = groups_x * groups_y
+    lanes = -(-experts // LANES) * LANES
+    count_row = jnp.pad(counts.reshape(1, experts).astype(jnp.float32), ((0, 0), (0, lanes - experts)))
+    owner_row = jnp.pad(new_owner.reshape(1, experts), ((0, 0), (0, lanes - experts)), constant_values=-1)
+    tile = (1, rows * groups_y, old_master.shape[2])
+    vmem = pl.BlockSpec(memory_space=pltpu.VMEM)
+    smem = pl.BlockSpec(memory_space=pltpu.SMEM)
+    hbm = pl.BlockSpec(memory_space=pl.ANY)
+    buffers = [pltpu.VMEM((experts, SUBLANES, width), jnp.float32)] * (2 * chunks)
+    master, first, second, count = pl.pallas_call(
+        functools.partial(rehome_kernel, dims),
+        out_shape=[jax.ShapeDtypeStruct(tile, jnp.float32)] * 3 + [jax.ShapeDtypeStruct((1, LANES), jnp.float32)],
+        in_specs=[smem, smem, vmem, vmem, hbm, hbm, hbm],
+        out_specs=[vmem] * 4,
+        scratch_shapes=buffers
+        + [
+            pltpu.SMEM((experts,), jnp.int32),
+            pltpu.VMEM((devices, 1, lanes), jnp.float32),
+            pltpu.SemaphoreType.DMA((chunks,)),
+            pltpu.SemaphoreType.DMA((chunks, groups_x)),
+            pltpu.SemaphoreType.DMA((chunks, groups_x)),
+            pltpu.SemaphoreType.DMA((chunks,)),
+            pltpu.SemaphoreType.DMA((chunks,)),
+            pltpu.SemaphoreType.DMA,
+            pltpu.SemaphoreType.DMA,
+        ],
+        compiler_params=pltpu.CompilerParams(collective_id=0, has_side_effects=True),
+    )(old_owner, new_owner, owner_row, count_row, old_master, old_first, old_second)
+    return adam_step(master, first, second, new_grad, count[0, 0])
+
+
+def body(old_master, old_first, old_second, new_grad, counts, old_owner, new_owner):
+    dims = tiled_plan(lax.axis_size("gx"), lax.axis_size("gy"), old_master.shape, old_owner.shape[0])
+    if dims is None:
+        return plain_body(old_master, old_first, old_second, new_grad, counts, old_owner, new_owner)
+    return kernel_body(dims, old_master, old_first, old_second, new_grad, counts, old_owner, new_owner)
 
 
 def solution(mesh):
@@ -59,10 +252,6 @@
         body,
         mesh=mesh,
         in_specs=placed,
-        out_specs=(
-            P(("gx", "gy"), None, None),
-            P(("gx", "gy"), None, None),
-            P(("gx", "gy"), None, None),
-        ),
+        out_specs=(P(("gx", "gy"), None, None),) * 3,
         check_vma=False,
     )

time: 157 us -> 73.4 us (0.47)
  blocking collectives: 94.3 us -> 0 us
  Pallas kernels: 0 us -> 66.7 us
  waiting for transfers between devices: 26.7 us -> 0 us
  starting transfers between devices: 14.1 us -> 0 us
  local copies, waits for them, and re-layouts: 14.8 us -> 2.4 us
  other arithmetic: 5.31 us -> 3.45 us
    pallas_call x0 -> x1, Pallas kernels: none -> 66.7 us  [kernel_body(): pl.pallas_call(functools.partial(rehome_kernel, dims), out_shape=[jax.Sha...]
    all_to_all x2 -> x0, blocking collectives: 51.2 us -> none  [body(): lax.all_to_all(permuted, ('gx', 'gy'), split_axis=0, concat_axis=1, tiled...]
    psum x1 -> x0, blocking collectives: 43.1 us -> none  [body(): totals = lax.psum(local_counts, ('gx', 'gy'))]
    all_to_all x4 -> x0, waiting for transfers between devices: 26.7 us -> none  [the longest x1 10.3 us: body(): lax.all_to_all(old_master, 'gx', split_axis=1, concat_axis=0, tiled=True)]
    all_to_all x4 -> x0, starting transfers between devices: 14.1 us -> none  [the longest x1 4.4 us: body(): lax.all_to_all(old_master, 'gx', split_axis=1, concat_axis=0, tiled=True)]
    gather x3 -> x0, local copies, waits for them, and re-layouts: 4.19 us -> none  [body(): permuted = tuple((jnp.take(state, source, axis=0) for state in by_rows))]
    unnamed x15 -> x8, local copies, waits for them, and re-layouts: 5.34 us -> 1.37 us
    all_to_all x7 -> x0, local copies, waits for them, and re-layouts: 2.82 us -> none  [the longest x2 1.44 us: body(): lax.all_to_all(old_first, 'gx', split_axis=1, concat_axis=0, tiled=True)]
  transfers between devices with their start and end apart: 4 -> 0, of which waited for: 3 -> 0; matrix products, arithmetic and copies ran while one was open for 7% -> 0% of each run, Pallas kernels for 0% -> 0%
where the time goes in v1:
time: 73.4 us; the launch traced here: 73.3 us
  Pallas kernels  66.7 us (91%)
  other arithmetic  3.45 us (5%)
  local copies, waits for them, and re-layouts  2.4 us (3%)
    pallas_call x1, Pallas kernels, kernel_body(): pl.pallas_call(functools.partial(rehome_kernel, dims), out_shape=[jax.Sha...  66.7 us
    sub x1, other arithmetic, adam_step(): new_master = master - 0.01 * (step_dir + 0.1 * master)  3.45 us

profile of v1, /device:TPU:0, one launch (start us, length us, event | category | flops | bytes accessed | tf_op | source)
XLA Modules:
  0.0 73.3 jit_solution(17731075600101604263)
XLA Ops:
  0.6 0.0 copy-start.3
  0.6 0.6 copy-done.3
  1.3 0.0 copy-start.1
  1.3 0.5 pad.9.count_row
  1.8 0.1 copy-done.1
  1.9 0.5 pad.8.owner_row
  2.5 0.0 copy-start
  2.5 66.7 %shard_map.94 = (f32[1,128,1536]{2,1,0:T(8,128)}, f32[1,128,1536]{2,1,0:T(8,128)}, f32[1,128,1536]{2,1,0:T(8,128)}, f32[1,128]{1,0:T(1,128)}) custom-call(s32[32]{0:T(128)} %old_owner.1, s32[32]{0:T(128)} %new_owner.1, s32[1,128]{1,0:T(1,128)} %pad.8.owner_row, f32[1,128]{1,0:T(1,128)} %pad.9.count_row, f32[8,16,1536]{2,1,0:T(8,128)} %old_m.1, ...), custom_call_target="tpu_custom_call" | custom-call | tf_op jit(solution)/shard_map/pallas_call | solution.py:212
  69.2 0.0 copy-start.2
  69.2 0.0 copy-done
  69.2 0.6 copy-done.2
  69.8 3.4 %multiply_subtract_fusion = (f32[1,128,1536]{2,1,0:T(8,128)}, f32[1,128,1536]{2,1,0:T(8,128)}, f32[1,128,1536]{2,1,0:T(8,128)}) fusion(f32[1,128,1536]{2,1,0:T(8,128)} %get-tuple-element.7, f32[]{:T(128)S(1)} %bitcast.6, bf16[1,128,1536]{2,1,0:T(8,128)(2,1)S(1)} %copy-done, f32[1,128,1536]{2,1,0:T(8,128)} %get-tuple-element.8, ...), kind=kLoop, calls=%fused_computation.2 | loop fusion | flops 3342336 | bytes 5111812 | tf_op jit(solution)/shard_map/sub | solution.py:23
  (1 shorter events, 0.0 us)
Async XLA Ops:
  0.6 0.7 copy-start.3
  1.3 0.7 copy-start.1
  2.5 66.8 %copy-start = (bf16[1,128,1536]{2,1,0:T(8,128)(2,1)S(1)}, bf16[1,128,1536]{2,1,0:T(8,128)(2,1)}, u32[]{:S(2)}) copy-start(bf16[1,128,1536]{2,1,0:T(8,128)(2,1)} %param.10) | copy-start | bytes 1179652
  69.2 0.6 copy-start.2

commit v2 on v1

--- a/solution.py
+++ b/solution.py
@@ -11,8 +11,8 @@
 second_correction = 1.0 - 0.999**10
 MESH = pl.DeviceIdType.MESH
 LANES = 128
+VMEM_GRANT = 8 << 20
 SUBLANES = 8
-SUBCHUNKS = 2
 
 
 def adam_step(master, first, second, grad, slot_count):
@@ -52,17 +52,19 @@
     return adam_step(arrived[0], arrived[1], arrived[2], new_grad, slot_count)
 
 
-def rehome_kernel(dims, old_owner, new_owner, owner_row, count_row, old_m, old_f, old_s, *rest):
-    groups_x, groups_y, experts, held, rows, tiles, width, chunks = dims
+def rehome_kernel(dims, old_owner_hbm, new_owner_hbm, owner_row_hbm, count_row, old_m, old_f, old_s, *rest):
+    groups_x, groups_y, experts, held, rows, tiles, span, pieces = dims
+    chunks = len(pieces)
     outs, count_out = rest[:3], rest[3]
     by_rows = rest[4 : 4 + chunks]
     staged = rest[4 + chunks : 4 + 2 * chunks]
-    (source, all_counts, local_sem, send1, recv1, send2, recv2, send_c, recv_c) = rest[4 + 2 * chunks :]
+    (
+        source, old_owner, new_owner, owner_row, all_counts, small_sem, local_sem, self_sem,
+        send1, recv1, send2, recv2, send_c, recv_c,
+    ) = rest[4 + 2 * chunks :]
     olds = (old_m, old_f, old_s)
     devices = groups_x * groups_y
-    per_state = chunks // 3
     splits = groups_x // tiles
-    span = per_state * width
     gx = lax.axis_index("gx")
     gy = lax.axis_index("gy")
     me = gx * groups_y + gy
@@ -83,14 +85,23 @@
         lax.fori_loop(0, devices - groups_x, step, 0)
         lax.fori_loop(devices - groups_x + 1, devices, step, 0)
 
+    small = (
+        pltpu.make_async_copy(old_owner_hbm, old_owner, small_sem.at[0]),
+        pltpu.make_async_copy(new_owner_hbm, new_owner, small_sem.at[1]),
+        pltpu.make_async_copy(owner_row_hbm, owner_row, small_sem.at[2]),
+        pltpu.make_async_copy(count_row, all_counts.at[me], small_sem.at[3]),
+    )
+    for copy in small:
+        copy.start()
+
     barrier = pltpu.get_barrier_semaphore()
     for_peers(lambda px, py: pl.semaphore_signal(barrier, inc=1, device_id=(px, py), device_id_type=MESH))
     pl.semaphore_wait(barrier, devices - 1)
 
     def old_piece(chunk, part):
-        state, sub = chunk // per_state, chunk % per_state
+        state, start, width = pieces[chunk]
         row = pl.multiple_of((part // splits) * SUBLANES, SUBLANES)
-        col = pl.multiple_of((part % splits) * span + sub * width, LANES)
+        col = pl.multiple_of((part % splits) * span + start, LANES)
         return olds[state].at[:, pl.ds(row, SUBLANES), pl.ds(col, width)]
 
     def own_rows(chunk):
@@ -110,7 +121,7 @@
     def local_copy(chunk):
         return pltpu.make_async_copy(old_piece(chunk, gx), own_rows(chunk), local_sem.at[chunk])
 
-    order = [sub + state * per_state for sub in range(per_state) for state in range(3)]
+    order = range(chunks)
     for chunk in order:
         for off in range(1, groups_x):
             first_copy(chunk, off).start()
@@ -127,7 +138,8 @@
         )
 
     for_peers(lambda px, py: count_copy(px, py).start())
-    all_counts[me] = count_row[...]
+    for copy in small:
+        copy.wait()
 
     def find(slot, carry):
         total = jnp.int32(0)
@@ -138,11 +150,14 @@
 
     lax.fori_loop(0, experts, find, 0)
 
-    def place(chunk):
-        state, sub = chunk // per_state, chunk % per_state
+    def landing(chunk):
+        state, start, width = pieces[chunk]
         row = pl.multiple_of(gy * rows + (gx // splits) * SUBLANES, SUBLANES)
-        col = pl.multiple_of((gx % splits) * span + sub * width, LANES)
-        return state, row, col
+        col = pl.multiple_of((gx % splits) * span + start, LANES)
+        return outs[state].at[0, pl.ds(row, SUBLANES), pl.ds(col, width)]
+
+    def self_copy(chunk):
+        return pltpu.make_async_copy(staged[chunk].at[me], landing(chunk), self_sem.at[chunk])
 
     for chunk in order:
         local_copy(chunk).wait()
@@ -154,12 +169,11 @@
             return carry
 
         lax.fori_loop(0, experts, stage, 0, unroll=4)
-        state, row, col = place(chunk)
 
         def send(px, py):
             pltpu.make_async_remote_copy(
                 src_ref=staged[chunk].at[px * groups_y + py],
-                dst_ref=outs[state].at[0, pl.ds(row, SUBLANES), pl.ds(col, width)],
+                dst_ref=landing(chunk),
                 send_sem=send2.at[chunk],
                 recv_sem=recv2.at[chunk],
                 device_id=(px, py),
@@ -167,11 +181,11 @@
             ).start()
 
         for_peers(send)
-        outs[state][0, pl.ds(row, SUBLANES), pl.ds(col, width)] = by_rows[chunk][source[me]]
+        self_copy(chunk).start()
 
     others = all_counts.at[pl.ds(0, devices - 1)]
     pltpu.make_async_copy(others, others, recv_c).wait()
-    totals = jnp.sum(all_counts[...], axis=0)
+    totals = jnp.sum(all_counts[...].astype(jnp.float32), axis=0)
     count = jnp.sum(jnp.where(owner_row[...] == me, totals, 0.0), axis=1, keepdims=True)
     count_out[...] = jnp.broadcast_to(count, count_out.shape)
 
@@ -180,6 +194,7 @@
             first_copy(chunk, off).wait_send()
     pltpu.make_async_copy(others, others, send_c).wait()
     for chunk in order:
+        self_copy(chunk).wait()
         sent = staged[chunk].at[pl.ds(0, devices - 1)]
         pltpu.make_async_copy(sent, sent, send2.at[chunk]).wait()
         pltpu.make_async_copy(sent, sent, recv2.at[chunk]).wait()
@@ -193,31 +208,39 @@
     if groups_x % tiles:
         return None
     span = cols // (groups_x // tiles)
-    if span % (LANES * SUBCHUNKS) or cols % span:
+    if span % LANES:
         return None
-    return (groups_x, groups_y, experts, held, rows, tiles, span // SUBCHUNKS, 3 * SUBCHUNKS)
+    half = (span // LANES + 1) // 2 * LANES
+    pieces = [(state, 0, half) for state in range(3)]
+    if half < span:
+        pieces += [(state, half, span - half) for state in range(3)]
+    if half > LANES:
+        pieces[:1] = [(0, 0, LANES), (0, LANES, half - LANES)]
+    return (groups_x, groups_y, experts, held, rows, tiles, span, tuple(pieces))
 
 
 def kernel_body(dims, old_master, old_first, old_second, new_grad, counts, old_owner, new_owner):
-    groups_x, groups_y, experts, held, rows, tiles, width, chunks = dims
+    groups_x, groups_y, experts, held, rows, tiles, span, pieces = dims
     devices = groups_x * groups_y
-    lanes = -(-experts // LANES) * LANES
-    count_row = jnp.pad(counts.reshape(1, experts).astype(jnp.float32), ((0, 0), (0, lanes - experts)))
-    owner_row = jnp.pad(new_owner.reshape(1, experts), ((0, 0), (0, lanes - experts)), constant_values=-1)
+    chunks = len(pieces)
     tile = (1, rows * groups_y, old_master.shape[2])
     vmem = pl.BlockSpec(memory_space=pltpu.VMEM)
-    smem = pl.BlockSpec(memory_space=pltpu.SMEM)
-    hbm = pl.BlockSpec(memory_space=pl.ANY)
-    buffers = [pltpu.VMEM((experts, SUBLANES, width), jnp.float32)] * (2 * chunks)
+    anywhere = pl.BlockSpec(memory_space=pl.ANY)
+    buffers = [pltpu.VMEM((experts, SUBLANES, width), jnp.float32) for _, _, width in pieces] * 2
     master, first, second, count = pl.pallas_call(
         functools.partial(rehome_kernel, dims),
         out_shape=[jax.ShapeDtypeStruct(tile, jnp.float32)] * 3 + [jax.ShapeDtypeStruct((1, LANES), jnp.float32)],
-        in_specs=[smem, smem, vmem, vmem, hbm, hbm, hbm],
-        out_specs=[vmem] * 4,
+        in_specs=[pl.BlockSpec(memory_space=pltpu.HBM)] * 7,
+        out_specs=[anywhere] * 3 + [vmem],
         scratch_shapes=buffers
         + [
             pltpu.SMEM((experts,), jnp.int32),
-            pltpu.VMEM((devices, 1, lanes), jnp.float32),
+            pltpu.SMEM((experts,), jnp.int32),
+            pltpu.SMEM((experts,), jnp.int32),
+            pltpu.VMEM((1, experts), jnp.int32),
+            pltpu.VMEM((devices, 1, experts), jnp.int32),
+            pltpu.SemaphoreType.DMA((4,)),
+            pltpu.SemaphoreType.DMA((chunks,)),
             pltpu.SemaphoreType.DMA((chunks,)),
             pltpu.SemaphoreType.DMA((chunks, groups_x)),
             pltpu.SemaphoreType.DMA((chunks, groups_x)),
@@ -226,8 +249,16 @@
             pltpu.SemaphoreType.DMA,
             pltpu.SemaphoreType.DMA,
         ],
-        compiler_params=pltpu.CompilerParams(collective_id=0, has_side_effects=True),
-    )(old_owner, new_owner, owner_row, count_row, old_master, old_first, old_second)
+        compiler_params=pltpu.CompilerParams(collective_id=0, has_side_effects=True, vmem_limit_bytes=VMEM_GRANT),
+    )(
+        old_owner,
+        new_owner,
+        new_owner.reshape(1, experts),
+        counts.reshape(1, experts),
+        old_master,
+        old_first,
+        old_second,
+    )
     return adam_step(master, first, second, new_grad, count[0, 0])
 
 

time: 73.4 us -> 70 us (0.954)
  Pallas kernels: 66.7 us -> 63.1 us
  local copies, waits for them, and re-layouts: 2.4 us -> 4.06 us
  other arithmetic: 3.45 us -> 1.86 us
    pallas_call x1, Pallas kernels: 66.7 us -> 63.1 us  [kernel_body(): pl.pallas_call(functools.partial(rehome_kernel, dims), out_shape=[jax.Sha...]
    unnamed x8 -> x14, local copies, waits for them, and re-layouts: 1.37 us -> 4.06 us
    sub x1, other arithmetic: 3.45 us -> 1.86 us  [adam_step(): new_master = master - 0.01 * (step_dir + 0.1 * master)]
    pad x2 -> x0, local copies, waits for them, and re-layouts: 1.03 us -> none  [the longest x1 0.52 us: kernel_body(): jnp.pad(counts.reshape(1, experts).astype(jnp.float32), ((0, 0), (0, lane...]
where the time goes in v2:
time: 70 us; the launch traced here: 69.7 us
  Pallas kernels  63.1 us (90%)
  local copies, waits for them, and re-layouts  4.06 us (6%)
  other arithmetic  1.86 us (3%)
    pallas_call x1, Pallas kernels, kernel_body(): pl.pallas_call(functools.partial(rehome_kernel, dims), out_shape=[jax.Sha...  63.1 us
    unnamed x14, local copies, waits for them, and re-layouts  4.06 us
    sub x1, other arithmetic, adam_step(): new_master = master - 0.01 * (step_dir + 0.1 * master)  1.86 us

profile of v2, /device:TPU:0, one launch (start us, length us, event | category | flops | bytes accessed | tf_op | source)
XLA Modules:
  0.0 69.7 jit_solution(17648830192753287698)
XLA Ops:
  0.6 0.0 copy-start.3
  0.6 0.0 copy-start.4
  0.7 0.0 copy-start.5
  0.7 0.6 copy-done.3
  1.3 0.0 copy-done.4
  1.3 0.0 copy-done.5
  1.3 0.0 copy-start
  1.3 1.1 %copy-done = f32[8,16,1536]{2,1,0:T(8,128)S(1)} copy-done((f32[8,16,1536]{2,1,0:T(8,128)S(1)}, f32[8,16,1536]{2,1,0:T(8,128)}, u32[]{:S(2)}) %copy-start) | copy-done | bytes 786456
  2.5 0.0 copy-start.1
  2.5 1.1 %copy-done.1 = f32[8,16,1536]{2,1,0:T(8,128)S(1)} copy-done((f32[8,16,1536]{2,1,0:T(8,128)S(1)}, f32[8,16,1536]{2,1,0:T(8,128)}, u32[]{:S(2)}) %copy-start.1) | copy-done | bytes 786456
  3.6 0.0 copy-start.2
  3.6 1.1 %copy-done.2 = f32[8,16,1536]{2,1,0:T(8,128)S(1)} copy-done((f32[8,16,1536]{2,1,0:T(8,128)S(1)}, f32[8,16,1536]{2,1,0:T(8,128)}, u32[]{:S(2)}) %copy-start.2) | copy-done | bytes 786456
  4.7 0.0 copy-start.6
  4.7 63.1 %shard_map.94 = (f32[1,128,1536]{2,1,0:T(8,128)S(1)}, f32[1,128,1536]{2,1,0:T(8,128)S(1)}, f32[1,128,1536]{2,1,0:T(8,128)S(1)}, f32[1,128]{1,0:T(1,128)S(1)}) custom-call(s32[32]{0:T(128)S(1)} %copy-done.4, s32[32]{0:T(128)S(1)} %copy-done.3, s32[1,32]{1,0:T(1,128)S(1)} %bitcast.4, s32[1,32]{1,0:T(1,128)S(1)} %bitcast.5, f32[8,16,1536]{2,1,0:T(8,128)S(1)} %copy-done, ...), custom_call_target="tpu_custom_call" | custom-call | tf_op jit(solution)/shard_map/pallas_call | solution.py:230
  67.9 0.0 copy-done.6
  67.9 1.9 %multiply_subtract_fusion = (f32[1,128,1536]{2,1,0:T(8,128)}, f32[1,128,1536]{2,1,0:T(8,128)}, f32[1,128,1536]{2,1,0:T(8,128)}) fusion(f32[1,128,1536]{2,1,0:T(8,128)S(1)} %get-tuple-element.7, f32[]{:T(128)S(1)} %bitcast.6, bf16[1,128,1536]{2,1,0:T(8,128)(2,1)S(1)} %copy-done.6, f32[1,128,1536]{2,1,0:T(8,128)S(1)} %get-tuple-element.8, ...), kind=kLoop, calls=%fused_computation.2 | loop fusion | flops 3342336 | bytes 5111812 | tf_op jit(solution)/shard_map/sub | solution.py:23
Async XLA Ops:
  0.6 0.7 copy-start.3
  0.6 0.7 copy-start.4
  0.7 0.7 copy-start.5
  1.3 1.1 %copy-start = (f32[8,16,1536]{2,1,0:T(8,128)S(1)}, f32[8,16,1536]{2,1,0:T(8,128)}, u32[]{:S(2)}) copy-start(f32[8,16,1536]{2,1,0:T(8,128)} %old_m.1) | copy-start | bytes 2359300
  2.5 1.1 %copy-start.1 = (f32[8,16,1536]{2,1,0:T(8,128)S(1)}, f32[8,16,1536]{2,1,0:T(8,128)}, u32[]{:S(2)}) copy-start(f32[8,16,1536]{2,1,0:T(8,128)} %old_f.1) | copy-start | bytes 2359300
  3.6 1.1 %copy-start.2 = (f32[8,16,1536]{2,1,0:T(8,128)S(1)}, f32[8,16,1536]{2,1,0:T(8,128)}, u32[]{:S(2)}) copy-start(f32[8,16,1536]{2,1,0:T(8,128)} %old_s.1) | copy-start | bytes 2359300
  4.7 63.1 %copy-start.6 = (bf16[1,128,1536]{2,1,0:T(8,128)(2,1)S(1)}, bf16[1,128,1536]{2,1,0:T(8,128)(2,1)}, u32[]{:S(2)}) copy-start(bf16[1,128,1536]{2,1,0:T(8,128)(2,1)} %param.10) | copy-start | bytes 1179652

commit v3 on v2

--- a/solution.py
+++ b/solution.py
@@ -11,7 +11,7 @@
 second_correction = 1.0 - 0.999**10
 MESH = pl.DeviceIdType.MESH
 LANES = 128
-VMEM_GRANT = 8 << 20
+VMEM_GRANT = 10 << 20
 SUBLANES = 8
 
 
@@ -58,10 +58,11 @@
     outs, count_out = rest[:3], rest[3]
     by_rows = rest[4 : 4 + chunks]
     staged = rest[4 + chunks : 4 + 2 * chunks]
+    ready = rest[4 + 2 * chunks : 4 + 3 * chunks]
     (
         source, old_owner, new_owner, owner_row, all_counts, small_sem, local_sem, self_sem,
         send1, recv1, send2, recv2, send_c, recv_c,
-    ) = rest[4 + 2 * chunks :]
+    ) = rest[4 + 3 * chunks :]
     olds = (old_m, old_f, old_s)
     devices = groups_x * groups_y
     splits = groups_x // tiles
@@ -69,21 +70,15 @@
     gy = lax.axis_index("gy")
     me = gx * groups_y + gy
 
-    def peer(i):
-        at = i // groups_x
-        sign = 1 - 2 * (at % 2)
-        off = groups_y // 2 + sign * ((at + 1) // 2)
-        px = (gx + i % groups_x) % groups_x
-        py = (gy + off) % groups_y
-        return px, py
+    peers_x = [(gx + off) % groups_x for off in range(groups_x)]
+    offsets = sorted(range(groups_y), key=lambda off: (-min(off, groups_y - off), off))
+    peers_y = {off: (gy + off) % groups_y for off in offsets}
 
     def for_peers(fn):
-        def step(i, carry):
-            fn(*peer(i))
-            return carry
-
-        lax.fori_loop(0, devices - groups_x, step, 0)
-        lax.fori_loop(devices - groups_x + 1, devices, step, 0)
+        for off_y in offsets:
+            for off_x in range(groups_x):
+                if off_x or off_y:
+                    fn(peers_x[off_x], peers_y[off_y])
 
     small = (
         pltpu.make_async_copy(old_owner_hbm, old_owner, small_sem.at[0]),
@@ -91,12 +86,11 @@
         pltpu.make_async_copy(owner_row_hbm, owner_row, small_sem.at[2]),
         pltpu.make_async_copy(count_row, all_counts.at[me], small_sem.at[3]),
     )
+    barrier = pltpu.get_barrier_semaphore()
+    for_peers(lambda px, py: pl.semaphore_signal(barrier, inc=1, device_id=(px, py), device_id_type=MESH))
+
     for copy in small:
         copy.start()
-
-    barrier = pltpu.get_barrier_semaphore()
-    for_peers(lambda px, py: pl.semaphore_signal(barrier, inc=1, device_id=(px, py), device_id_type=MESH))
-    pl.semaphore_wait(barrier, devices - 1)
 
     def old_piece(chunk, part):
         state, start, width = pieces[chunk]
@@ -107,25 +101,46 @@
     def own_rows(chunk):
         return by_rows[chunk].at[pl.ds(gx * held, held)]
 
+    def local_copy(chunk, off):
+        target = own_rows(chunk) if off == 0 else ready[chunk].at[off - 1]
+        return pltpu.make_async_copy(old_piece(chunk, peers_x[off]), target, local_sem.at[chunk, off])
+
     def first_copy(chunk, off):
-        part = (gx + off) % groups_x
         return pltpu.make_async_remote_copy(
-            src_ref=old_piece(chunk, part),
+            src_ref=ready[chunk].at[off - 1],
             dst_ref=own_rows(chunk),
             send_sem=send1.at[chunk, off],
             recv_sem=recv1.at[chunk, off],
-            device_id=(part, gy),
+            device_id=(peers_x[off], gy),
             device_id_type=MESH,
         )
 
-    def local_copy(chunk):
-        return pltpu.make_async_copy(old_piece(chunk, gx), own_rows(chunk), local_sem.at[chunk])
-
     order = range(chunks)
     for chunk in order:
+        for off in [*range(1, groups_x), 0]:
+            local_copy(chunk, off).start()
+
+    for copy in small:
+        copy.wait()
+
+    owners = [new_owner[e] for e in range(experts)]
+    places = [old_owner[e] for e in range(experts)]
+
+    def find(slot, carry):
+        total = jnp.int32(0)
+        for e in range(experts):
+            total = total + jnp.where(owners[e] == slot, places[e], 0)
+        source[slot] = total
+        return carry
+
+    lax.fori_loop(0, experts, find, 0)
+
+    pl.semaphore_wait(barrier, devices - 1)
+
+    for chunk in order:
         for off in range(1, groups_x):
+            local_copy(chunk, off).wait()
             first_copy(chunk, off).start()
-        local_copy(chunk).start()
 
     def count_copy(px, py):
         return pltpu.make_async_remote_copy(
@@ -138,18 +153,6 @@
         )
 
     for_peers(lambda px, py: count_copy(px, py).start())
-    for copy in small:
-        copy.wait()
-
-    def find(slot, carry):
-        total = jnp.int32(0)
-        for e in range(experts):
-            total = total + jnp.where(new_owner[e] == slot, old_owner[e], 0)
-        source[slot] = total
-        return carry
-
-    lax.fori_loop(0, experts, find, 0)
-
     def landing(chunk):
         state, start, width = pieces[chunk]
         row = pl.multiple_of(gy * rows + (gx // splits) * SUBLANES, SUBLANES)
@@ -160,7 +163,7 @@
         return pltpu.make_async_copy(staged[chunk].at[me], landing(chunk), self_sem.at[chunk])
 
     for chunk in order:
-        local_copy(chunk).wait()
+        local_copy(chunk, 0).wait()
         for off in range(1, groups_x):
             first_copy(chunk, off).wait_recv()
 
@@ -227,6 +230,10 @@
     vmem = pl.BlockSpec(memory_space=pltpu.VMEM)
     anywhere = pl.BlockSpec(memory_space=pl.ANY)
     buffers = [pltpu.VMEM((experts, SUBLANES, width), jnp.float32) for _, _, width in pieces] * 2
+    buffers += [pltpu.VMEM((groups_x - 1, held, SUBLANES, width), jnp.float32) for _, _, width in pieces]
+    row = new_owner.reshape(1, experts)
+    operands = (old_owner, new_owner, row, counts.reshape(1, experts), old_master, old_first, old_second)
+    kept = [pltpu.with_memory_space_constraint(array, pltpu.HBM) for array in operands]
     master, first, second, count = pl.pallas_call(
         functools.partial(rehome_kernel, dims),
         out_shape=[jax.ShapeDtypeStruct(tile, jnp.float32)] * 3 + [jax.ShapeDtypeStruct((1, LANES), jnp.float32)],
@@ -240,7 +247,7 @@
             pltpu.VMEM((1, experts), jnp.int32),
             pltpu.VMEM((devices, 1, experts), jnp.int32),
             pltpu.SemaphoreType.DMA((4,)),
-            pltpu.SemaphoreType.DMA((chunks,)),
+            pltpu.SemaphoreType.DMA((chunks, groups_x)),
             pltpu.SemaphoreType.DMA((chunks,)),
             pltpu.SemaphoreType.DMA((chunks, groups_x)),
             pltpu.SemaphoreType.DMA((chunks, groups_x)),
@@ -250,15 +257,7 @@
             pltpu.SemaphoreType.DMA,
         ],
         compiler_params=pltpu.CompilerParams(collective_id=0, has_side_effects=True, vmem_limit_bytes=VMEM_GRANT),
-    )(
-        old_owner,
-        new_owner,
-        new_owner.reshape(1, experts),
-        counts.reshape(1, experts),
-        old_master,
-        old_first,
-        old_second,
-    )
+    )(*kept)
     return adam_step(master, first, second, new_grad, count[0, 0])
 
 

time: 70 us -> 66.4 us (0.949)
  local copies, waits for them, and re-layouts: 4.06 us -> 0.01 us
    unnamed x14 -> x2, local copies, waits for them, and re-layouts: 4.06 us -> 0.01 us
where the time goes in v3:
time: 66.4 us; the launch traced here: 66.2 us
  Pallas kernels  63.7 us (96%)
  other arithmetic  1.86 us (3%)
    pallas_call x1, Pallas kernels, kernel_body(): pl.pallas_call(functools.partial(rehome_kernel, dims), out_shape=[jax.Sha...  63.7 us
    sub x1, other arithmetic, adam_step(): new_master = master - 0.01 * (step_dir + 0.1 * master)  1.86 us

profile of v3, /device:TPU:0, one launch (start us, length us, event | category | flops | bytes accessed | tf_op | source)
XLA Modules:
  0.0 66.2 jit_solution(9371251770080221574)
XLA Ops:
  0.6 0.0 copy-start
  0.6 63.7 %shard_map.94 = (f32[1,128,1536]{2,1,0:T(8,128)S(1)}, f32[1,128,1536]{2,1,0:T(8,128)S(1)}, f32[1,128,1536]{2,1,0:T(8,128)S(1)}, f32[1,128]{1,0:T(1,128)S(1)}) custom-call(s32[32]{0:T(128)} %old_owner_hbm.1, s32[32]{0:T(128)} %new_owner_hbm.1, s32[1,32]{1,0:T(1,128)} %bitcast.5, s32[1,32]{1,0:T(1,128)} %bitcast.6, f32[8,16,1536]{2,1,0:T(8,128)} %old_m.1, ...), custom_call_target="tpu_custom_call" | custom-call | tf_op jit(solution)/shard_map/pallas_call | solution.py:237
  64.3 0.0 copy-done
  64.3 1.9 %multiply_subtract_fusion = (f32[1,128,1536]{2,1,0:T(8,128)}, f32[1,128,1536]{2,1,0:T(8,128)}, f32[1,128,1536]{2,1,0:T(8,128)}) fusion(f32[1,128,1536]{2,1,0:T(8,128)S(1)} %get-tuple-element.7, f32[]{:T(128)S(1)} %bitcast.4, bf16[1,128,1536]{2,1,0:T(8,128)(2,1)S(1)} %copy-done, f32[1,128,1536]{2,1,0:T(8,128)S(1)} %get-tuple-element.8, ...), kind=kLoop, calls=%fused_computation.2 | loop fusion | flops 3342336 | bytes 5111812 | tf_op jit(solution)/shard_map/sub | solution.py:23
Async XLA Ops:
  0.6 63.7 %copy-start = (bf16[1,128,1536]{2,1,0:T(8,128)(2,1)S(1)}, bf16[1,128,1536]{2,1,0:T(8,128)(2,1)}, u32[]{:S(2)}) copy-start(bf16[1,128,1536]{2,1,0:T(8,128)(2,1)} %param.10) | copy-start | bytes 1179652

commit v4 on v3

--- a/solution.py
+++ b/solution.py
@@ -61,7 +61,7 @@
     ready = rest[4 + 2 * chunks : 4 + 3 * chunks]
     (
         source, old_owner, new_owner, owner_row, all_counts, small_sem, local_sem, self_sem,
-        send1, recv1, send2, recv2, send_c, recv_c,
+        send1, recv1, send2, recv2, send_c, recv_c, row_in,
     ) = rest[4 + 3 * chunks :]
     olds = (old_m, old_f, old_s)
     devices = groups_x * groups_y
@@ -87,7 +87,10 @@
         pltpu.make_async_copy(count_row, all_counts.at[me], small_sem.at[3]),
     )
     barrier = pltpu.get_barrier_semaphore()
-    for_peers(lambda px, py: pl.semaphore_signal(barrier, inc=1, device_id=(px, py), device_id_type=MESH))
+    for off_y in offsets[:-1]:
+        pl.semaphore_signal(barrier, inc=1, device_id=(gx, peers_y[off_y]), device_id_type=MESH)
+    for off_x in range(1, groups_x):
+        pl.semaphore_signal(barrier, inc=1, device_id=(peers_x[off_x], gy), device_id_type=MESH)
 
     for copy in small:
         copy.start()
@@ -120,6 +123,15 @@
         for off in [*range(1, groups_x), 0]:
             local_copy(chunk, off).start()
 
+    pl.semaphore_wait(barrier, groups_x + groups_y - 2)
+    for off_x in range(1, groups_x):
+        pl.semaphore_signal(row_in, inc=1, device_id=(peers_x[off_x], gy), device_id_type=MESH)
+
+    for chunk in order:
+        for off in range(1, groups_x):
+            local_copy(chunk, off).wait()
+            first_copy(chunk, off).start()
+
     for copy in small:
         copy.wait()
 
@@ -134,13 +146,6 @@
         return carry
 
     lax.fori_loop(0, experts, find, 0)
-
-    pl.semaphore_wait(barrier, devices - 1)
-
-    for chunk in order:
-        for off in range(1, groups_x):
-            local_copy(chunk, off).wait()
-            first_copy(chunk, off).start()
 
     def count_copy(px, py):
         return pltpu.make_async_remote_copy(
@@ -152,7 +157,7 @@
             device_id_type=MESH,
         )
 
-    for_peers(lambda px, py: count_copy(px, py).start())
+    pl.semaphore_wait(row_in, groups_x - 1)
     def landing(chunk):
         state, start, width = pieces[chunk]
         row = pl.multiple_of(gy * rows + (gx // splits) * SUBLANES, SUBLANES)
@@ -185,6 +190,8 @@
 
         for_peers(send)
         self_copy(chunk).start()
+        if chunk == 0:
+            for_peers(lambda px, py: count_copy(px, py).start())
 
     others = all_counts.at[pl.ds(0, devices - 1)]
     pltpu.make_async_copy(others, others, recv_c).wait()
@@ -255,6 +262,7 @@
             pltpu.SemaphoreType.DMA((chunks,)),
             pltpu.SemaphoreType.DMA,
             pltpu.SemaphoreType.DMA,
+            pltpu.SemaphoreType.REGULAR,
         ],
         compiler_params=pltpu.CompilerParams(collective_id=0, has_side_effects=True, vmem_limit_bytes=VMEM_GRANT),
     )(*kept)

time: 66.4 us -> 65.2 us (0.982)
  Pallas kernels: 63.7 us -> 62.5 us
    pallas_call x1, Pallas kernels: 63.7 us -> 62.5 us  [kernel_body(): pl.pallas_call(functools.partial(rehome_kernel, dims), out_shape=[jax.Sha...]
where the time goes in v4:
time: 65.2 us; the launch traced here: 65 us
  Pallas kernels  62.5 us (96%)
  other arithmetic  1.86 us (3%)
  between operations  0.66 us (1%)
    pallas_call x1, Pallas kernels, kernel_body(): pl.pallas_call(functools.partial(rehome_kernel, dims), out_shape=[jax.Sha...  62.5 us
    sub x1, other arithmetic, adam_step(): new_master = master - 0.01 * (step_dir + 0.1 * master)  1.86 us

profile of v4, /device:TPU:0, one launch (start us, length us, event | category | flops | bytes accessed | tf_op | source)
XLA Modules:
  0.0 65.0 jit_solution(12420123918295719389)
XLA Ops:
  0.6 0.0 copy-start
  0.6 62.5 %shard_map.94 = (f32[1,128,1536]{2,1,0:T(8,128)S(1)}, f32[1,128,1536]{2,1,0:T(8,128)S(1)}, f32[1,128,1536]{2,1,0:T(8,128)S(1)}, f32[1,128]{1,0:T(1,128)S(1)}) custom-call(s32[32]{0:T(128)} %old_owner_hbm.1, s32[32]{0:T(128)} %new_owner_hbm.1, s32[1,32]{1,0:T(1,128)} %bitcast.5, s32[1,32]{1,0:T(1,128)} %bitcast.6, f32[8,16,1536]{2,1,0:T(8,128)} %old_m.1, ...), custom_call_target="tpu_custom_call" | custom-call | tf_op jit(solution)/shard_map/pallas_call | solution.py:244
  63.1 0.0 copy-done
  63.1 1.9 %multiply_subtract_fusion = (f32[1,128,1536]{2,1,0:T(8,128)}, f32[1,128,1536]{2,1,0:T(8,128)}, f32[1,128,1536]{2,1,0:T(8,128)}) fusion(f32[1,128,1536]{2,1,0:T(8,128)S(1)} %get-tuple-element.7, f32[]{:T(128)S(1)} %bitcast.4, bf16[1,128,1536]{2,1,0:T(8,128)(2,1)S(1)} %copy-done, f32[1,128,1536]{2,1,0:T(8,128)S(1)} %get-tuple-element.8, ...), kind=kLoop, calls=%fused_computation.2 | loop fusion | flops 3342336 | bytes 5111812 | tf_op jit(solution)/shard_map/sub | solution.py:23
Async XLA Ops:
  0.6 62.5 %copy-start = (bf16[1,128,1536]{2,1,0:T(8,128)(2,1)S(1)}, bf16[1,128,1536]{2,1,0:T(8,128)(2,1)}, u32[]{:S(2)}) copy-start(bf16[1,128,1536]{2,1,0:T(8,128)(2,1)} %param.10) | copy-start | bytes 1179652

commit v5 on v4

--- a/solution.py
+++ b/solution.py
@@ -225,7 +225,8 @@
     if half < span:
         pieces += [(state, half, span - half) for state in range(3)]
     if half > LANES:
-        pieces[:1] = [(0, 0, LANES), (0, LANES, half - LANES)]
+        rest = [(state, LANES, half - LANES) for state in range(3)]
+        pieces[:3] = [(state, 0, LANES) for state in range(3)] + rest
     return (groups_x, groups_y, experts, held, rows, tiles, span, tuple(pieces))
 
 

time: 65.2 us -> 64.7 us (level)
  no operation moved by 1% of the time
where the time goes in v5:
time: 64.7 us; the launch traced here: 64.5 us
  Pallas kernels  62 us (96%)
  other arithmetic  1.86 us (3%)
  between operations  0.66 us (1%)
    pallas_call x1, Pallas kernels, kernel_body(): pl.pallas_call(functools.partial(rehome_kernel, dims), out_shape=[jax.Sha...  62 us
    sub x1, other arithmetic, adam_step(): new_master = master - 0.01 * (step_dir + 0.1 * master)  1.86 us

profile of v5, /device:TPU:0, one launch (start us, length us, event | category | flops | bytes accessed | tf_op | source)
XLA Modules:
  0.0 64.5 jit_solution(4223175562248832508)
XLA Ops:
  0.6 0.0 copy-start
  0.6 62.0 %shard_map.94 = (f32[1,128,1536]{2,1,0:T(8,128)S(1)}, f32[1,128,1536]{2,1,0:T(8,128)S(1)}, f32[1,128,1536]{2,1,0:T(8,128)S(1)}, f32[1,128]{1,0:T(1,128)S(1)}) custom-call(s32[32]{0:T(128)} %old_owner_hbm.1, s32[32]{0:T(128)} %new_owner_hbm.1, s32[1,32]{1,0:T(1,128)} %bitcast.5, s32[1,32]{1,0:T(1,128)} %bitcast.6, f32[8,16,1536]{2,1,0:T(8,128)} %old_m.1, ...), custom_call_target="tpu_custom_call" | custom-call | tf_op jit(solution)/shard_map/pallas_call | solution.py:245
  62.6 0.0 copy-done
  62.7 1.9 %multiply_subtract_fusion = (f32[1,128,1536]{2,1,0:T(8,128)}, f32[1,128,1536]{2,1,0:T(8,128)}, f32[1,128,1536]{2,1,0:T(8,128)}) fusion(f32[1,128,1536]{2,1,0:T(8,128)S(1)} %get-tuple-element.7, f32[]{:T(128)S(1)} %bitcast.4, bf16[1,128,1536]{2,1,0:T(8,128)(2,1)S(1)} %copy-done, f32[1,128,1536]{2,1,0:T(8,128)S(1)} %get-tuple-element.8, ...), kind=kLoop, calls=%fused_computation.2 | loop fusion | flops 3342336 | bytes 5111812 | tf_op jit(solution)/shard_map/sub | solution.py:23
Async XLA Ops:
  0.6 62.0 %copy-start = (bf16[1,128,1536]{2,1,0:T(8,128)(2,1)S(1)}, bf16[1,128,1536]{2,1,0:T(8,128)(2,1)}, u32[]{:S(2)}) copy-start(bf16[1,128,1536]{2,1,0:T(8,128)(2,1)} %param.10) | copy-start | bytes 1179652
